TPU v7x, 32 devices: a whole 2x2x4 slice. The times are simulated.
32 devices in a mesh: grp: 2 (over x), spec: 16 (over z, y, core).
Axes of the slice: x: 2, y: 2, z: 4, core: 2. Of those that a mesh axis runs over, the one named last changes fastest.
Arguments:
- spectrum: float32 [3072, 1536], P(('grp', 'spec')), parts along dimension 0, may hold values from 0.05 to 5
- sea_mask: int32 [1536], replicated, may hold values from 0 to 1, as said below
- wind_speed: float32 [3072], P('grp'), parts along dimension 0, may hold values from 0.3 to 3
- wind_angle: float32 [3072], P('grp'), parts along dimension 0, may hold values from -3.140625 to 3.140625
Outputs:
- new_spectrum: float32 [3072, 1536], P(('grp', 'spec')), parts along dimension 0
- wave_height: float32 [3072], P(('grp', 'spec')), parts along dimension 0
- mean_height: float32 [2], P('grp'), parts along dimension 0
There are 2 independent parts, one for each index of `grp`. A program takes and returns all parts, laid end to end along the dimension named above; an argument that names none is the same for every part. Nothing has to cross between parts.
Inputs may be any that keep to these rules, and one draw needn't show every extreme that they name: `sea_mask`: exactly 1024 cells are sea.
All inputs are finite; a program needn't handle non-finite values.
Results may differ from a plain program's by a relative error of at most 0.00002.
Values sent between devices are 32-bit elements; how exact they have to be, the bound alone decides.
A program may use at most 64 MiB of HBM per device.

v0:
```python
import math

import jax
import jax.numpy as jnp
from jax import lax
from jax.sharding import PartitionSpec as P

NF = 48
ND = 32
NLON = 384
ADV_STEPS = 2
SEA_DEV = 64


def upwind_step(energy, courant_x, courant_y, sea_grid):
    west_cell = jnp.roll(energy, 1, axis=2)
    east_cell = jnp.roll(energy, -1, axis=2)
    edge_row = jnp.zeros_like(energy[:, :1])
    south_cell = jnp.concatenate([edge_row, energy[:, :-1]], axis=1)
    north_cell = jnp.concatenate([energy[:, 1:], edge_row], axis=1)
    updated = (
        energy
        - jnp.maximum(courant_x, 0.0) * (energy - west_cell)
        - jnp.minimum(courant_x, 0.0) * (east_cell - energy)
        - jnp.maximum(courant_y, 0.0) * (energy - south_cell)
        - jnp.minimum(courant_y, 0.0) * (north_cell - energy)
    )
    return updated * sea_grid


def courant_numbers(freq_index, dir_index, lat_count, dir_count):
    speed = 0.2 * jnp.exp(-math.log(1.1) * freq_index)
    heading = 2.0 * math.pi * (dir_index + 0.5) / dir_count
    rows = jnp.arange(lat_count, dtype=jnp.float32)
    latitude = (-75.0 + 150.0 * (rows + 0.5) / lat_count) * (math.pi / 180.0)
    courant_x = (speed * jnp.cos(heading))[:, None, None] / jnp.cos(latitude)[None, :, None]
    courant_y = (speed * jnp.sin(heading))[:, None, None]
    return (courant_x, courant_y)


def shift_freq(values, amount):
    if amount > 0:
        filler = jnp.zeros_like(values[:amount])
        return jnp.concatenate([filler, values[:-amount]], axis=0)
    filler = jnp.zeros_like(values[:-amount])
    return jnp.concatenate([values[-amount:], filler], axis=0)


def source_terms(energy, speed, angle):
    freq_count = energy.shape[0]
    dir_count = energy.shape[1]
    freq_ids = jnp.arange(freq_count, dtype=jnp.float32)
    frequency = jnp.exp(math.log(1.1) * (freq_ids - freq_count // 2))[:, None, None]
    heading = (2.0 * math.pi * (jnp.arange(dir_count, dtype=jnp.float32) + 0.5) / dir_count)[
        None, :, None
    ]
    energy_mean = jnp.mean(energy, axis=(0, 1))
    moment_one = jnp.mean(frequency * energy, axis=(0, 1))
    mean_freq = moment_one / (energy_mean + 1e-06)
    steepness = energy_mean * mean_freq * mean_freq
    breaking = steepness * steepness / (1.0 + steepness * steepness)
    wind_gain = (
        0.05
        * frequency
        * jnp.maximum(
            0.0, speed[None, None, :] * frequency * jnp.cos(heading - angle[None, None, :]) - 1.0
        )
    )
    damping = 0.03 * frequency * breaking[None, None, :]
    valid = ((freq_ids >= 3) & (freq_ids <= freq_count - 3)).astype(jnp.float32)[:, None, None]
    interaction = jnp.zeros_like(energy)
    for mirror in (1, -1):
        plus_bins = shift_freq(jnp.roll(energy, -mirror, axis=1), -2)
        minus_bins = shift_freq(jnp.roll(energy, 3 * mirror, axis=1), 3)
        transfer_rate = (
            0.001
            * valid
            * (energy * energy * (plus_bins + minus_bins) - 2.0 * energy * plus_bins * minus_bins)
        )
        interaction = interaction - 2.0 * transfer_rate
        interaction = interaction + jnp.roll(shift_freq(transfer_rate, 2), mirror, axis=1)
        interaction = interaction + jnp.roll(shift_freq(transfer_rate, -3), -3 * mirror, axis=1)
    updated = energy + (wind_gain - damping) * energy + interaction
    raw_height = 4.0 * jnp.sqrt(jnp.mean(updated, axis=(0, 1)) + 1e-06)
    return (updated, raw_height)


def local(spectrum, sea_mask, wind_speed, wind_angle):
    count = lax.axis_size("spec")
    position = lax.axis_index("spec")
    bins_dev = spectrum.shape[0]
    cells = spectrum.shape[1]
    points = cells // count
    lat_count = cells // NLON
    sea_float = sea_mask.astype(jnp.float32)
    bin_ids = position * bins_dev + jnp.arange(bins_dev, dtype=jnp.int32)
    freq_index = (bin_ids // ND).astype(jnp.float32)
    dir_index = (bin_ids % ND).astype(jnp.float32)
    courant_x, courant_y = courant_numbers(freq_index, dir_index, lat_count, ND)
    sea_grid = sea_float.reshape(1, lat_count, NLON)
    energy = (spectrum * sea_float[None, :]).reshape(bins_dev, lat_count, NLON)
    for substep in range(ADV_STEPS):
        energy = upwind_step(energy, courant_x, courant_y, sea_grid)
    advected = energy.reshape(bins_dev, cells)
    outgoing = advected.reshape(bins_dev, count, points)
    arrived = lax.all_to_all(outgoing, "spec", split_axis=1, concat_axis=0, tiled=True)
    start = position * points
    speed_own = lax.dynamic_slice_in_dim(wind_speed, start, points)
    angle_own = lax.dynamic_slice_in_dim(wind_angle, start, points)
    sea_own = lax.dynamic_slice_in_dim(sea_float, start, points)
    updated, raw_height = source_terms(arrived.reshape(NF, ND, points), speed_own, angle_own)
    wave_height = sea_own * raw_height
    own_total = jnp.zeros((count, 1), jnp.float32) + jnp.sum(wave_height)
    returned, totals = (
        lax.all_to_all(
            updated.reshape(NF * ND, 1, points), "spec", split_axis=0, concat_axis=1, tiled=True
        ),
        lax.all_to_all(own_total, "spec", split_axis=0, concat_axis=1, tiled=True),
    )
    new_spectrum = returned.reshape(bins_dev, cells)
    height_sum = jnp.sum(totals)
    mean_height = (height_sum / (SEA_DEV * count)).reshape(1)
    return (new_spectrum, wave_height, mean_height)


def solution(mesh):
    in_specs = (P(("grp", "spec"), None), P(), P("grp"), P("grp"))
    out_specs = (P(("grp", "spec"), None), P(("grp", "spec")), P("grp"))
    return jax.shard_map(local, mesh=mesh, in_specs=in_specs, out_specs=out_specs, check_vma=False)
```

profile of v0, /device:TPU:0, one launch (start us, length us, event | category | flops | bytes accessed | tf_op | source)
XLA Modules:
  0.0 82.3 jit_solution(3236672330348931112)
XLA Ops:
  0.7 0.1 broadcast_maximum_fusion.1
  0.8 0.1 cosine_multiply_fusion
  0.8 0.5 copy-done
  1.3 1.1 %broadcast_multiply_fusion = f32[96,1536]{1,0:T(8,128)S(1)} fusion(f32[96,1536]{1,0:T(8,128)} %param.4, f32[1536]{0:T(1024)S(1)} %convert_element_type.31), kind=kLoop, calls=%fused_computation.43 | loop fusion | flops 147456 | bytes 1185792 | tf_op jit(solution)/shard_map/mul | solution.py:101
  2.5 0.2 reshape.287
  2.7 0.2 fusion.36
  2.8 0.2 fusion.34
  3.1 0.4 fusion.35
  3.4 0.1 broadcast_maximum_fusion
  3.5 0.1 copy.25
  3.6 0.1 copy.26
  3.7 1.4 %fusion.11 = f32[96,4,384]{2,1,0:T(4,128)S(1)} fusion(f32[96,4,384]{2,1,0:T(4,128)S(1)} %reshape.287, f32[96,4,383]{2,1,0:T(4,128)S(1)} %get-tuple-element.26, f32[96,4,1]{2,1,0:T(4,128)S(1)} %get-tuple-element.28, f32[96,4,1]{2,1,0:T(4,128)S(1)} %get-tuple-element.27, f32[96,4,383]{2,1,0:T(4,128)S(1)} %get-tuple-element.25, ...), kind=kLoop, calls=%fused_computation.31 | loop fusion | flops 2211840 | bytes 3254016 | tf_op jit(solution)/shard_map/mul | solution.py:28
  5.2 0.2 fusion.33
  5.3 0.2 fusion.31
  5.6 0.4 fusion.32
  5.9 1.4 %fusion.18 = f32[96,4,384]{2,1,0:T(4,128)S(1)} fusion(f32[96,4,384]{2,1,0:T(4,128)S(1)} %fusion.11, f32[96,4,383]{2,1,0:T(4,128)S(1)} %get-tuple-element.20, f32[96,4,1]{2,1,0:T(4,128)S(1)} %get-tuple-element.22, f32[96,4,1]{2,1,0:T(4,128)S(1)} %get-tuple-element.21, f32[96,4,383]{2,1,0:T(4,128)S(1)} %get-tuple-element.19, ...), kind=kLoop, calls=%fused_computation.40 | loop fusion | flops 2211840 | bytes 3254016 | tf_op jit(solution)/shard_map/mul | solution.py:28
  7.3 0.3 reshape_reshape.3
  7.7 1.1 %copy.27 = f32[96,16,96]{2,0,1:T(8,128)} copy(f32[96,16,96]{2,1,0:T(8,128)S(1)} %reshape_reshape.3) | data formatting | bytes 1179648 | tf_op jit(solution)/shard_map/reshape;reshape | solution.py:105
  8.8 7.4 %all-to-all-start = ((f32[96,16,96]{2,0,1:T(8,128)}), f32[96,16,96]{2,0,1:T(8,128)S(1)}, u32[]{:S(2)}, u32[]{:S(2)}) async-start(f32[96,16,96]{2,0,1:T(8,128)} %copy.27), calls=%async_computation | async-start | bytes 1572864 | tf_op jit(solution)/shard_map/all_to_all | solution.py:106
  16.2 0.8 dynamic_slice.9
  17.0 0.8 dynamic_slice.10
  17.8 0.1 mul.397
  17.9 0.1 mul.398
  18.0 0.1 subtract_cosine_fusion
  18.2 0.1 broadcast_multiply_fusion.2
  18.2 16.7 %all-to-all-done = f32[96,16,96]{2,0,1:T(8,128)S(1)} async-done(((f32[96,16,96]{2,0,1:T(8,128)}), f32[96,16,96]{2,0,1:T(8,128)S(1)}, u32[]{:S(2)}, u32[]{:S(2)}) %all-to-all-start) | async-done | bytes 589856 | tf_op jit(solution)/shard_map/all_to_all | solution.py:106
  35.0 0.1 fusion.29
  35.1 0.2 fusion.28
  35.3 0.7 subtract_multiply_fusion.1
  36.1 0.1 pad_slice_fusion.3
  36.2 0.1 slice.179
  36.3 1.0 %pad_slice_fusion = f32[48,29,96]{2,1,0:T(8,128)} fusion(f32[45,32,96]{2,1,0:T(8,128)S(1)} %slice.179), kind=kLoop, calls=%fused_computation.17 | loop fusion | bytes 1087488 | tf_op jit(solution)/shard_map/jit(_roll_static)/slice | solution.py:82
  37.3 0.1 slice.172
  37.4 1.0 %pad_slice_fusion.6 = f32[48,31,96]{2,1,0:T(8,128)} fusion(f32[46,32,96]{2,1,0:T(8,128)S(1)} %slice.172), kind=kLoop, calls=%fused_computation.23 | loop fusion | bytes 1136640 | tf_op jit(solution)/shard_map/jit(_roll_static)/slice | solution.py:81
  38.4 1.0 %pad_slice_fusion.5 = f32[48,31,96]{2,1,0:T(8,128)} fusion(f32[46,32,96]{2,1,0:T(8,128)S(1)} %slice.178), kind=kLoop, calls=%fused_computation.22 | loop fusion | bytes 1136640 | tf_op jit(solution)/shard_map/jit(_roll_static)/slice | solution.py:81
  39.4 0.3 fusion.5
  39.7 0.2 reduce_sum.45
  39.9 0.1 broadcast_multiply_fusion.1
  40.0 3.4 %fusion.25 = (f32[96]{0:T(128)S(1)}, f32[48,32,96]{2,1,0:T(8,128)}) fusion(f32[48,29,96]{2,1,0:T(8,128)} %pad_slice_fusion, f32[48,3,96]{2,1,0:T(4,128)S(1)} %pad_slice_fusion.1, f32[48,1,96]{2,1,0:T(1,128)S(1)} %pad_slice_fusion.4, f32[48,31,96]{2,1,0:T(8,128)} %pad_slice_fusion.5, f32[48,32,96]{2,1,0:T(8,128)S(1)} %get-tuple-element.8, ...), kind=kLoop, calls=%fused_computation.76 | loop fusion | flops 3096480 | bytes 4768320 | tf_op jit(solution)/shard_map/reduce_sum | solution.py:84
  43.4 1.2 %fusion.24 = (f32[]{:T(128)}, f32[96]{0:T(128)}) fusion(f32[96]{0:T(128)S(1)} %get-tuple-element.5, f32[1536]{0:T(1024)S(1)} %convert_element_type.31, s32[]{:T(128)S(6)} %select_n.39), kind=kLoop, calls=%fused_computation.75 | loop fusion | flops 479 | bytes 1160 | tf_op jit(solution)/shard_map/reduce_sum | solution.py:113
  44.6 0.6 add.195
  45.3 11.6 %all_to_all.40 = f32[16,1,1]{2,1,0:T(1,128)S(1)} all-to-all(f32[16,1,1]{2,1,0:T(1,128)S(1)} %add.195), channel_id=1, replica_groups=mesh['grp'=2,'spec'=16] {'spec'}, dimensions={0} | all-to-all | bytes 128 | tf_op jit(solution)/shard_map/all_to_all | solution.py:118
  56.9 3.6 %all-to-all-start.1 = ((f32[1536,1,96]{2,1,0:T(1,128)}), f32[1536,1,96]{2,1,0:T(1,128)S(1)}, u32[]{:S(2)}, u32[]{:S(2)}) async-start(f32[1536,1,96]{2,1,0:T(1,128)} %bitcast.6), calls=%async_computation.1 | async-start | bytes 1572864 | tf_op jit(solution)/shard_map/all_to_all | solution.py:115
  60.5 0.6 reduce_sum.49
  61.8 17.4 %all-to-all-done.1 = f32[1536,1,96]{2,1,0:T(1,128)S(1)} async-done(((f32[1536,1,96]{2,1,0:T(1,128)}), f32[1536,1,96]{2,1,0:T(1,128)S(1)}, u32[]{:S(2)}, u32[]{:S(2)}) %all-to-all-start.1) | async-done | bytes 589856 | tf_op jit(solution)/shard_map/all_to_all | solution.py:115
  79.1 0.4 copy.32
  79.5 0.5 copy.30
  80.1 1.1 %reshape.290 = f32[96,1536]{1,0:T(8,128)} reshape(f32[96,16,1,96]{3,1,0,2:T(8,128)S(1)} %copy.30) | data formatting | bytes 1179648 | tf_op jit(solution)/shard_map/reshape | solution.py:120
  (19 shorter events, 0.4 us)
Async XLA Ops:
  0.6 0.7 copy-start
  8.8 26.1 %all-to-all-start = ((f32[96,16,96]{2,0,1:T(8,128)}), f32[96,16,96]{2,0,1:T(8,128)S(1)}, u32[]{:S(2)}, u32[]{:S(2)}) async-start(f32[96,16,96]{2,0,1:T(8,128)} %copy.27), calls=%async_computation | async-start | bytes 1572864 | tf_op jit(solution)/shard_map/all_to_all | solution.py:106
  56.9 22.3 %all-to-all-start.1 = ((f32[1536,1,96]{2,1,0:T(1,128)}), f32[1536,1,96]{2,1,0:T(1,128)S(1)}, u32[]{:S(2)}, u32[]{:S(2)}) async-start(f32[1536,1,96]{2,1,0:T(1,128)} %bitcast.6), calls=%async_computation.1 | async-start | bytes 1572864 | tf_op jit(solution)/shard_map/all_to_all | solution.py:115
where the time goes:
time: 83 us; the launch traced here: 82.3 us
  waiting for transfers between devices  34 us (41%)
  local copies, waits for them, and re-layouts  12 us (14%)
  blocking collectives  11.6 us (14%)
  other arithmetic  11 us (13%)
  starting transfers between devices  11 us (13%)
  between operations  2.67 us (3%)
    all_to_all x1, waiting for transfers between devices, local(): lax.all_to_all(updated.reshape(NF * ND, 1, points), 'spec', split_axis=0,...  17.4 us
    all_to_all x1, waiting for transfers between devices, local(): lax.all_to_all(outgoing, 'spec', split_axis=1, concat_axis=0, tiled=True)  16.7 us
    all_to_all x1, blocking collectives, local(): lax.all_to_all(own_total, 'spec', split_axis=0, concat_axis=1, tiled=True)  11.6 us
    all_to_all x1, starting transfers between devices, local(): lax.all_to_all(outgoing, 'spec', split_axis=1, concat_axis=0, tiled=True)  7.41 us
    all_to_all x1, starting transfers between devices, local(): lax.all_to_all(updated.reshape(NF * ND, 1, points), 'spec', split_axis=0,...  3.61 us
    reduce_sum x1, other arithmetic, source_terms(): raw_height = 4.0 * jnp.sqrt(jnp.mean(updated, axis=(0, 1)) + 1e-06)  3.39 us
    mul x2, other arithmetic, upwind_step(): return updated * sea_grid  2.82 us
    slice x4, local copies, waits for them, and re-layouts, source_terms(): jnp.roll(shift_freq(transfer_rate, 2), mirror, axis=1)  2.01 us
  transfers between devices with their start and end apart: 2, of which 2 were waited for; matrix products, arithmetic and copies ran while one was open for 3% of the time, Pallas kernels for 0%

commit v1 on v0

--- a/solution.py
+++ b/solution.py
@@ -1,8 +1,11 @@
+import functools
 import math
 
 import jax
 import jax.numpy as jnp
 from jax import lax
+from jax.experimental import pallas as pl
+from jax.experimental.pallas import tpu as pltpu
 from jax.sharding import PartitionSpec as P
 
 NF = 48
@@ -123,7 +126,413 @@
     return (new_spectrum, wave_height, mean_height)
 
 
+HALO = 5
+LANES = 128
+
+
+def group_size(count, bins_dev, cells):
+    size = 4
+    if count % size or bins_dev % ND or cells % (size * LANES) or cells % NLON:
+        return 0
+    if NLON % LANES or bins_dev // ND * size < 2 * HALO or cells % count:
+        return 0
+    return size
+
+
+def fused_kernel(
+    count, group, aux_ref, spec_ref, out_ref, wave_ref, mean_ref,
+    raw, adv, held, done, mom_out, mom_in, wind, acc, sum_out, sum_in,
+    load_sem, held_sem, y_sem, up_sem, down_sem, mom_send, mom_recv,
+    ret_send, ret_recv, sum_send, sum_recv,
+):
+    f32 = jnp.float32
+    bins_dev, cells = adv.shape
+    freq_dev = bins_dev // ND
+    freq_group = freq_dev * group
+    width = cells // group
+    zones = count // group
+    lat_count = cells // NLON
+    sides = group // 2
+    me = lax.axis_index("spec")
+    zone, rank = me // group, me % group
+    side, core = rank // 2, rank % 2
+
+    def remote(src, dst, send, recv, target):
+        return pltpu.make_async_remote_copy(
+            src_ref=src, dst_ref=dst, send_sem=send, recv_sem=recv,
+            device_id={"spec": target}, device_id_type=pl.DeviceIdType.MESH,
+        )
+
+    barrier = pltpu.get_barrier_semaphore()
+    for step in range(1, count):
+        pl.semaphore_signal(
+            barrier, inc=1, device_id={"spec": (me + step) % count},
+            device_id_type=pl.DeviceIdType.MESH,
+        )
+    loads = [
+        pltpu.make_async_copy(
+            spec_ref.at[pl.ds(f * ND, ND)], raw.at[pl.ds(f * ND, ND)], load_sem.at[f]
+        )
+        for f in range(freq_dev)
+    ]
+    for load in loads:
+        load.start()
+
+    @pl.when(zone == 0)
+    def _():
+        held[0:HALO] = jnp.zeros((HALO, ND, width), f32)
+
+    @pl.when(zone == zones - 1)
+    def _():
+        held[HALO + freq_group :] = jnp.zeros((HALO, ND, width), f32)
+
+    dirs = lax.broadcasted_iota(jnp.int32, (ND, LANES), 0).astype(f32)
+    heading = 2.0 * math.pi * (dirs + 0.5) / ND
+    cos_h, sin_h = jnp.cos(heading), jnp.sin(heading)
+    log_step = math.log(1.1)
+    lats = [math.radians(-75.0 + 150.0 * (r + 0.5) / lat_count) for r in range(lat_count)]
+    sea = [aux_ref[0:1, r * NLON : (r + 1) * NLON] for r in range(lat_count)]
+    quarter = ND // 4
+    tiles = NLON // LANES
+    moments = [[jnp.zeros((quarter, NLON), f32) for _ in range(lat_count)] for _ in range(2)]
+    for f in range(freq_dev):
+        loads[f].wait()
+        freq = (me * freq_dev + f).astype(f32)
+        speed = 0.2 * jnp.exp(jnp.full((quarter, LANES), -log_step, f32) * freq)
+        omega = jnp.exp(jnp.full((quarter, LANES), log_step, f32) * (freq - NF // 2))
+        omega = jnp.concatenate([omega] * tiles, axis=1)
+        sums = [None] * lat_count
+        for q in range(4):
+            east, north = q in (0, 3), q in (0, 1)
+            rows = slice(f * ND + q * quarter, f * ND + (q + 1) * quarter)
+            part = slice(q * quarter, (q + 1) * quarter)
+            cx0 = speed * jnp.abs(cos_h[part])
+            cy = jnp.concatenate([speed * jnp.abs(sin_h[part])] * tiles, axis=1)
+            cx = [jnp.concatenate([cx0 * (1.0 / math.cos(a))] * tiles, axis=1) for a in lats]
+            energy = [raw[rows, r * NLON : (r + 1) * NLON] * sea[r] for r in range(lat_count)]
+            for _ in range(ADV_STEPS):
+                fresh = []
+                for r in range(lat_count):
+                    e = energy[r]
+                    side_x = pltpu.roll(e, 1 if east else NLON - 1, 1)
+                    other = r - 1 if north else r + 1
+                    side_y = energy[other] if 0 <= other < lat_count else 0.0
+                    fresh.append((e - cx[r] * (e - side_x) - cy * (e - side_y)) * sea[r])
+                energy = fresh
+            for r in range(lat_count):
+                adv[rows, r * NLON : (r + 1) * NLON] = energy[r]
+                sums[r] = energy[r] if q == 0 else sums[r] + energy[r]
+        for r in range(lat_count):
+            moments[0][r] = moments[0][r] + sums[r]
+            moments[1][r] = moments[1][r] + omega * sums[r]
+    for i in range(2):
+        for r in range(lat_count):
+            mom_out[i : i + 1, r * NLON : (r + 1) * NLON] = jnp.sum(
+                moments[i][r], axis=0, keepdims=True
+            )
+
+    pl.semaphore_wait(barrier, count - 1)
+
+    def cells_of(index):
+        return pl.ds(pl.multiple_of(index * width, LANES), width)
+
+    for step in range(1, count):
+        target = (me + step) % count
+        remote(
+            mom_out.at[:, cells_of(target % group)], mom_in.at[me],
+            mom_send.at[step - 1], mom_recv.at[me], target,
+        ).start()
+
+    offsets = [(dy, dc) for dy in range(sides) for dc in range(2)]
+
+    def rank_of(offset):
+        return (side + offset[0]) % sides * 2 + (core + offset[1]) % 2
+
+    def y_copy(f, i):
+        peer = rank_of(offsets[i])
+        return remote(
+            adv.at[pl.ds(f * ND, ND), cells_of(peer)], held.at[HALO + rank * freq_dev + f],
+            y_sem.at[i - 1, f], held_sem.at[HALO + rank * freq_dev + f], zone * group + peer,
+        )
+
+    def own_copy(f):
+        slot = HALO + rank * freq_dev + f
+        return pltpu.make_async_copy(
+            adv.at[pl.ds(f * ND, ND), cells_of(rank)], held.at[slot], held_sem.at[slot]
+        )
+
+    for f in range(freq_dev):
+        for i in list(range(2, group)) + [1]:
+            y_copy(f, i).start()
+        own_copy(f).start()
+    local_mom = pltpu.make_async_copy(
+        mom_out.at[:, cells_of(rank)], mom_in.at[me], mom_recv.at[me]
+    )
+    local_mom.start()
+
+    wind[...] = (
+        jnp.concatenate([cos_h] * (width // LANES), axis=1) * aux_ref[1:2, cells_of(rank)]
+        + jnp.concatenate([sin_h] * (width // LANES), axis=1) * aux_ref[2:3, cells_of(rank)]
+    )
+
+    def up_copy(slot):
+        return remote(
+            held.at[HALO + slot], held.at[HALO + slot - freq_group],
+            up_sem.at[slot - (freq_group - HALO)], held_sem.at[HALO + slot - freq_group],
+            (zone + 1) % zones * group + rank,
+        )
+
+    def down_copy(slot):
+        return remote(
+            held.at[HALO + slot], held.at[HALO + slot + freq_group],
+            down_sem.at[slot], held_sem.at[HALO + slot + freq_group],
+            (zone + zones - 1) % zones * group + rank,
+        )
+
+    def arrive(index):
+        remote(
+            held.at[index], held.at[index], up_sem.at[0], held_sem.at[index],
+            (me + 1) % count,
+        ).wait_recv()
+
+    for dy in range(sides):
+        for f in range(freq_dev):
+            for dc in range(2):
+                slot = rank_of((dy, dc)) * freq_dev + f
+                if (dy, dc) == (0, 0):
+                    own_copy(f).wait()
+                else:
+                    arrive(HALO + slot)
+
+                @pl.when((slot >= freq_group - HALO) & (zone < zones - 1))
+                def _():
+                    up_copy(slot).start()
+
+                @pl.when((slot < HALO) & (zone > 0))
+                def _():
+                    down_copy(slot).start()
+
+    local_mom.wait()
+    for step in range(1, count):
+        source = (me + step) % count
+        remote(
+            mom_in.at[source], mom_in.at[source], mom_send.at[0], mom_recv.at[source], source
+        ).wait_recv()
+    total = jnp.sum(mom_in[...], axis=0) * (1.0 / (NF * ND))
+    energy_mean, moment_one = total[0:1], total[1:2]
+    mean_freq = moment_one / (energy_mean + 1e-06)
+    steepness = energy_mean * mean_freq * mean_freq
+    breaking = steepness * steepness / (1.0 + steepness * steepness)
+
+    acc[...] = jnp.zeros_like(acc)
+    ascending = side > 0
+
+    for i in range(HALO):
+        early = jnp.where(ascending, i, HALO + freq_group + i)
+
+        @pl.when(jnp.where(ascending, zone > 0, zone < zones - 1))
+        def _():
+            arrive(early)
+
+    def ret_copy(k):
+        owner, f = k // freq_dev, k % freq_dev
+        return remote(
+            done.at[k],
+            out_ref.at[pl.ds(pl.multiple_of(f * ND, ND), ND), cells_of(rank)],
+            ret_send.at[k], ret_recv.at[rank, f], zone * group + owner,
+        )
+
+    def ret_local(k):
+        f = k % freq_dev
+        return pltpu.make_async_copy(
+            done.at[k],
+            out_ref.at[pl.ds(pl.multiple_of(f * ND, ND), ND), cells_of(rank)],
+            ret_recv.at[rank, f],
+        )
+
+    def source_step(i, carry):
+        k = jnp.where(ascending, i, freq_group - 1 - i)
+        late = i - (freq_group - HALO)
+
+        @pl.when((late >= 0) & jnp.where(ascending, zone < zones - 1, zone > 0))
+        def _():
+            arrive(jnp.where(ascending, HALO + freq_group + late, HALO - 1 - late))
+
+        freq = zone * freq_group + k
+
+        def scale(index, factor):
+            return jnp.where((index >= 3) & (index <= NF - 3), factor, 0.0).astype(f32)
+
+        w_own, w_low, w_high = scale(freq, -0.002), scale(freq - 2, 0.001), scale(freq + 3, 0.001)
+        omega = jnp.exp(
+            jnp.full((1, LANES), log_step, f32) * (freq.astype(f32) - NF // 2)
+        )
+        for t in range(width // LANES):
+            lanes = slice(t * LANES, (t + 1) * LANES)
+
+            def slab(shift):
+                return held[HALO + k + shift, :, lanes]
+
+            def turn(values, amount):
+                return pltpu.roll(values, amount % ND, 0)
+
+            def rate(a, p, m):
+                return a * (a * (p + m) - 2.0 * (p * m))
+
+            own = slab(0)
+            p2, m3, m2, m5, p3, p5 = (slab(s) for s in (2, -3, -2, -5, 3, 5))
+            near = rate(own, turn(p2, -1), turn(m3, 3)) + rate(own, turn(p2, 1), turn(m3, -3))
+            low = rate(turn(m2, 1), own, turn(m5, 4)) + rate(turn(m2, -1), own, turn(m5, -4))
+            high = rate(turn(p3, -3), turn(p5, -4), own) + rate(turn(p3, 3), turn(p5, 4), own)
+            interaction = w_own * near + w_low * low + w_high * high
+            gain = (0.05 * omega) * jnp.maximum(0.0, wind[:, lanes] * omega - 1.0)
+            damping = (0.03 * omega) * breaking[:, lanes]
+            fresh = own + (gain - damping) * own + interaction
+            done[k, :, lanes] = fresh
+            acc[:, lanes] += fresh
+
+        @pl.when(k // freq_dev == rank)
+        def _():
+            ret_local(k).start()
+
+        @pl.when(k // freq_dev != rank)
+        def _():
+            ret_copy(k).start()
+
+        return carry
+
+    lax.fori_loop(0, freq_group, source_step, 0)
+
+    sum_out[...] = jnp.sum(acc[...], axis=0, keepdims=True)
+
+    def sum_copy(step):
+        return remote(
+            sum_out, sum_in.at[me], sum_send.at[step - 1], sum_recv.at[me], (me + step) % count
+        )
+
+    for step in range(1, count):
+        sum_copy(step).start()
+    sum_in[me] = sum_out[...]
+    for step in range(1, count):
+        source = (me + step) % count
+        remote(
+            sum_out, sum_in.at[source], sum_send.at[0], sum_recv.at[source], source
+        ).wait_recv()
+
+    per_row = count // group
+    mine_row = me // per_row
+    height_sum = jnp.zeros((1, width), f32)
+    mine = jnp.zeros((1, width), f32)
+    for g in range(group):
+        mass = sum_in[g]
+        for other in range(1, zones):
+            mass = mass + sum_in[other * group + g]
+        sea_row = aux_ref[0:1, g * width : (g + 1) * width]
+        height = sea_row * (4.0 * jnp.sqrt(mass * (1.0 / (NF * ND)) + 1e-06))
+        height_sum = height_sum + height
+        mine = jnp.where(mine_row == g, height, mine)
+    points = cells // count
+    shift = (me % per_row) * points
+    turned = pltpu.roll(jnp.broadcast_to(mine, (8, width)), (width - shift) % width, 1)
+    wave_ref[...] = turned[0:1, :points]
+    mean_ref[...] = jnp.sum(height_sum, axis=1, keepdims=True) * (1.0 / (SEA_DEV * count))
+
+    for f in range(freq_dev):
+        for i in range(1, group):
+            peer = rank_of(offsets[i])
+            remote(
+                done.at[0], out_ref.at[pl.ds(f * ND, ND), cells_of(peer)],
+                ret_send.at[0], ret_recv.at[peer, f], zone * group + peer,
+            ).wait_recv()
+            y_copy(f, i).wait_send()
+            ret_copy(peer * freq_dev + f).wait_send()
+        ret_local(rank * freq_dev + f).wait()
+    for step in range(1, count):
+        remote(
+            mom_out.at[:, cells_of(0)], mom_in.at[me], mom_send.at[step - 1],
+            mom_recv.at[me], (me + step) % count,
+        ).wait_send()
+        sum_copy(step).wait_send()
+
+    @pl.when(zone < zones - 1)
+    def _():
+        for slot in range(freq_group - HALO, freq_group):
+            up_copy(slot).wait_send()
+
+    @pl.when(zone > 0)
+    def _():
+        for slot in range(HALO):
+            down_copy(slot).wait_send()
+
+
+def fused_local(spectrum, sea_mask, wind_speed, wind_angle):
+    count = lax.axis_size("spec")
+    bins_dev, cells = spectrum.shape
+    group = group_size(count, bins_dev, cells)
+    freq_dev = bins_dev // ND
+    freq_group = freq_dev * group
+    width = cells // group
+    points = cells // count
+    aux = jnp.stack(
+        [
+            sea_mask.astype(jnp.float32),
+            wind_speed * jnp.cos(wind_angle),
+            wind_speed * jnp.sin(wind_angle),
+        ]
+    )
+    f32 = jnp.float32
+    dma = pltpu.SemaphoreType.DMA
+    out, wave, mean = pl.pallas_call(
+        functools.partial(fused_kernel, count, group),
+        out_shape=(
+            jax.ShapeDtypeStruct((bins_dev, cells), f32),
+            jax.ShapeDtypeStruct((1, points), f32),
+            jax.ShapeDtypeStruct((1, 1), f32),
+        ),
+        in_specs=[
+            pl.BlockSpec(memory_space=pltpu.VMEM),
+            pl.BlockSpec(memory_space=pl.ANY),
+        ],
+        out_specs=(
+            pl.BlockSpec(memory_space=pl.ANY),
+            pl.BlockSpec(memory_space=pltpu.VMEM),
+            pl.BlockSpec(memory_space=pltpu.VMEM),
+        ),
+        scratch_shapes=[
+            pltpu.VMEM((bins_dev, cells), f32),
+            pltpu.VMEM((bins_dev, cells), f32),
+            pltpu.VMEM((freq_group + 2 * HALO, ND, width), f32),
+            pltpu.VMEM((freq_group, ND, width), f32),
+            pltpu.VMEM((2, cells), f32),
+            pltpu.VMEM((count, 2, width), f32),
+            pltpu.VMEM((ND, width), f32),
+            pltpu.VMEM((ND, width), f32),
+            pltpu.VMEM((1, width), f32),
+            pltpu.VMEM((count, 1, width), f32),
+            dma((freq_dev,)),
+            dma((freq_group + 2 * HALO,)),
+            dma((group - 1, freq_dev)),
+            dma((HALO,)),
+            dma((HALO,)),
+            dma((count - 1,)),
+            dma((count,)),
+            dma((freq_group,)),
+            dma((group, freq_dev)),
+            dma((count - 1,)),
+            dma((count,)),
+        ],
+        compiler_params=pltpu.CompilerParams(collective_id=0, has_side_effects=True),
+    )(aux, spectrum)
+    return (out, wave.reshape(points), mean.reshape(1))
+
+
 def solution(mesh):
     in_specs = (P(("grp", "spec"), None), P(), P("grp"), P("grp"))
     out_specs = (P(("grp", "spec"), None), P(("grp", "spec")), P("grp"))
-    return jax.shard_map(local, mesh=mesh, in_specs=in_specs, out_specs=out_specs, check_vma=False)
+
+    def body(spectrum, sea_mask, wind_speed, wind_angle):
+        fits = group_size(mesh.shape["spec"], *spectrum.shape)
+        plan = fused_local if fits else local
+        return plan(spectrum, sea_mask, wind_speed, wind_angle)
+
+    return jax.shard_map(body, mesh=mesh, in_specs=in_specs, out_specs=out_specs, check_vma=False)

time: 83 us -> 33.6 us (0.40)
  waiting for transfers between devices: 34 us -> 0 us
  Pallas kernels: 0 us -> 26.3 us
  blocking collectives: 11.6 us -> 0 us
  starting transfers between devices: 11 us -> 0 us
  other arithmetic: 11 us -> 1.38 us
  local copies, waits for them, and re-layouts: 12 us -> 3.13 us
    all_to_all x2 -> x0, waiting for transfers between devices: 34 us -> none  [the longest x1 17.4 us: local(): lax.all_to_all(updated.reshape(NF * ND, 1, points), 'spec', split_axis=0,...]
    pallas_call x0 -> x1, Pallas kernels: none -> 26.3 us  [fused_local(): pl.pallas_call(functools.partial(fused_kernel, count, group), out_shape=(...]
    all_to_all x1 -> x0, blocking collectives: 11.6 us -> none  [local(): lax.all_to_all(own_total, 'spec', split_axis=0, concat_axis=1, tiled=True)]
    all_to_all x2 -> x0, starting transfers between devices: 11 us -> none  [the longest x1 7.41 us: local(): lax.all_to_all(outgoing, 'spec', split_axis=1, concat_axis=0, tiled=True)]
    reduce_sum x5 -> x0, other arithmetic: 5.69 us -> none  [the longest x1 3.39 us: source_terms(): raw_height = 4.0 * jnp.sqrt(jnp.mean(updated, axis=(0, 1)) + 1e-06)]
    slice x22 -> x0, local copies, waits for them, and re-layouts: 5.21 us -> none  [the longest x4 2.01 us: source_terms(): jnp.roll(shift_freq(transfer_rate, 2), mirror, axis=1)]
    mul x10 -> x1, other arithmetic: 4.91 us -> 0.05 us  [fused_local(): wind_speed * jnp.cos(wind_angle)]
    unnamed x2 -> x8, local copies, waits for them, and re-layouts: 0.52 us -> 3.12 us
  transfers between devices with their start and end apart: 2 -> 0, of which waited for: 2 -> 0; matrix products, arithmetic and copies ran while one was open for 3% -> 0% of each run, Pallas kernels for 0% -> 0%
where the time goes in v1:
time: 33.6 us; the launch traced here: 33.3 us
  Pallas kernels  26.3 us (78%)
  local copies, waits for them, and re-layouts  3.13 us (9%)
  between operations  2.45 us (7%)
  other arithmetic  1.38 us (4%)
    pallas_call x1, Pallas kernels, fused_local(): pl.pallas_call(functools.partial(fused_kernel, count, group), out_shape=(...  26.3 us
    unnamed x8, local copies, waits for them, and re-layouts  3.12 us
    convert_element_type x1, other arithmetic, fused_local(): sea_mask.astype(jnp.float32)  0.71 us

profile of v1, /device:TPU:0, one launch (start us, length us, event | category | flops | bytes accessed | tf_op | source)
XLA Modules:
  0.0 33.3 jit_solution(11377735852475977603)
XLA Ops:
  0.6 0.0 copy-start.1
  0.6 0.7 %convert_element_type.3 = f32[1536]{0:T(1024)S(1)} convert(s32[1536]{0:T(1024)} %param.5) | non-fusion elementwise | flops 1536 | bytes 12288 | tf_op jit(solution)/shard_map/convert_element_type | solution.py:478
  1.3 0.0 copy-start
  1.4 0.0 copy-done.1
  1.4 0.7 %copy-done = f32[1536]{0:T(1024)S(1)} copy-done((f32[1536]{0:T(1024)S(1)}, f32[1536]{0:T(1024)}, u32[]{:S(2)}) %copy-start) | copy-done | bytes 6168
  2.0 0.1 cosine_multiply_fusion
  2.1 0.6 %pad_maximum_fusion.aux_ref = f32[3,1536]{1,0:T(4,128)} fusion(f32[1,1536]{1,0:T(1,128)S(1)} %stack.14, f32[1,1536]{1,0:T(1,128)S(1)} %stack.13, f32[1,1536]{1,0:T(1,128)S(1)} %stack.12), kind=kLoop, calls=%fused_computation | loop fusion | flops 9216 | bytes 36864 | tf_op jit(solution)/shard_map/stack | solution.py:476
  2.8 26.3 %shard_map.67 = (f32[96,1536]{1,0:T(8,128)}, f32[1,96]{1,0:T(1,128)}, f32[1,1]{1,0:T(1,128)}) custom-call(f32[3,1536]{1,0:T(4,128)} %pad_maximum_fusion.aux_ref, f32[96,1536]{1,0:T(8,128)} %spec_ref.1), custom_call_target="tpu_custom_call" | custom-call | tf_op jit(solution)/shard_map/pallas_call | solution.py:485
  29.1 0.0 copy-start.2
  29.1 1.9 %copy.10 = f32[96,1536]{1,0:T(8,128)} copy(f32[96,1536]{1,0:T(8,128)} %get-tuple-element.14) | data formatting | bytes 1179648
  31.0 0.0 copy-done.2
  31.0 0.5 %copy.11 = f32[96]{0:T(128)} copy(f32[96]{0:T(128)S(1)} %bitcast.2) | data formatting | bytes 768
  (3 shorter events, 0.0 us)
Async XLA Ops:
  0.6 0.7 %copy-start.1 = (f32[1536]{0:T(1024)S(1)}, f32[1536]{0:T(1024)}, u32[]{:S(2)}) copy-start(f32[1536]{0:T(1024)} %param.7) | copy-start | bytes 18436
  1.3 0.7 %copy-start = (f32[1536]{0:T(1024)S(1)}, f32[1536]{0:T(1024)}, u32[]{:S(2)}) copy-start(f32[1536]{0:T(1024)} %param.6) | copy-start | bytes 18436
  29.1 1.9 %copy-start.2 = (f32[1,96]{1,0:T(1,128)S(1)}, f32[1,96]{1,0:T(1,128)}, u32[]{:S(2)}) copy-start(f32[1,96]{1,0:T(1,128)} %get-tuple-element.7) | copy-start | bytes 1156

commit v2 on v1

--- a/solution.py
+++ b/solution.py
@@ -140,7 +140,8 @@
 
 
 def fused_kernel(
-    count, group, aux_ref, spec_ref, out_ref, wave_ref, mean_ref,
+    count, group, sea_in, wind_in, angle_in, spec_ref, out_ref, wave_ref, mean_ref,
+    sea_raw, wind_raw, aux_ref, aux_sem,
     raw, adv, held, done, mom_out, mom_in, wind, acc, sum_out, sum_in,
     load_sem, held_sem, y_sem, up_sem, down_sem, mom_send, mom_recv,
     ret_send, ret_recv, sum_send, sum_recv,
@@ -175,7 +176,12 @@
         )
         for f in range(freq_dev)
     ]
-    for load in loads:
+    small = [
+        pltpu.make_async_copy(sea_in, sea_raw, aux_sem.at[0]),
+        pltpu.make_async_copy(wind_in, wind_raw.at[0:1], aux_sem.at[1]),
+        pltpu.make_async_copy(angle_in, wind_raw.at[1:2], aux_sem.at[2]),
+    ]
+    for load in small[:1] + loads + small[1:]:
         load.start()
 
     @pl.when(zone == 0)
@@ -191,6 +197,8 @@
     cos_h, sin_h = jnp.cos(heading), jnp.sin(heading)
     log_step = math.log(1.1)
     lats = [math.radians(-75.0 + 150.0 * (r + 0.5) / lat_count) for r in range(lat_count)]
+    small[0].wait()
+    aux_ref[0:1] = sea_raw[...].astype(f32)
     sea = [aux_ref[0:1, r * NLON : (r + 1) * NLON] for r in range(lat_count)]
     quarter = ND // 4
     tiles = NLON // LANES
@@ -270,10 +278,12 @@
     )
     local_mom.start()
 
-    wind[...] = (
-        jnp.concatenate([cos_h] * (width // LANES), axis=1) * aux_ref[1:2, cells_of(rank)]
-        + jnp.concatenate([sin_h] * (width // LANES), axis=1) * aux_ref[2:3, cells_of(rank)]
-    )
+    small[1].wait()
+    small[2].wait()
+    speed_own, angle_own = wind_raw[0:1, cells_of(rank)], wind_raw[1:2, cells_of(rank)]
+    wind[...] = jnp.concatenate([cos_h] * (width // LANES), axis=1) * (
+        speed_own * jnp.cos(angle_own)
+    ) + jnp.concatenate([sin_h] * (width // LANES), axis=1) * (speed_own * jnp.sin(angle_own))
 
     def up_copy(slot):
         return remote(
@@ -473,32 +483,29 @@
     freq_group = freq_dev * group
     width = cells // group
     points = cells // count
-    aux = jnp.stack(
-        [
-            sea_mask.astype(jnp.float32),
-            wind_speed * jnp.cos(wind_angle),
-            wind_speed * jnp.sin(wind_angle),
-        ]
-    )
     f32 = jnp.float32
     dma = pltpu.SemaphoreType.DMA
     out, wave, mean = pl.pallas_call(
         functools.partial(fused_kernel, count, group),
         out_shape=(
-            jax.ShapeDtypeStruct((bins_dev, cells), f32),
+            pltpu.VMEM((bins_dev, cells), f32),
             jax.ShapeDtypeStruct((1, points), f32),
             jax.ShapeDtypeStruct((1, 1), f32),
         ),
         in_specs=[
+            pl.BlockSpec(memory_space=pl.ANY),
+        ]
+        * 4,
+        out_specs=(
             pl.BlockSpec(memory_space=pltpu.VMEM),
-            pl.BlockSpec(memory_space=pl.ANY),
-        ],
-        out_specs=(
-            pl.BlockSpec(memory_space=pl.ANY),
             pl.BlockSpec(memory_space=pltpu.VMEM),
             pl.BlockSpec(memory_space=pltpu.VMEM),
         ),
         scratch_shapes=[
+            pltpu.VMEM((1, cells), jnp.int32),
+            pltpu.VMEM((2, cells), f32),
+            pltpu.VMEM((1, cells), f32),
+            dma((3,)),
             pltpu.VMEM((bins_dev, cells), f32),
             pltpu.VMEM((bins_dev, cells), f32),
             pltpu.VMEM((freq_group + 2 * HALO, ND, width), f32),
@@ -522,7 +529,12 @@
             dma((count,)),
         ],
         compiler_params=pltpu.CompilerParams(collective_id=0, has_side_effects=True),
-    )(aux, spectrum)
+    )(
+        sea_mask.reshape(1, cells),
+        wind_speed.reshape(1, cells),
+        wind_angle.reshape(1, cells),
+        spectrum,
+    )
     return (out, wave.reshape(points), mean.reshape(1))
 
 

time: 33.6 us -> 33 us (0.982)
  local copies, waits for them, and re-layouts: 3.13 us -> 4.52 us
  other arithmetic: 1.38 us -> 0 us
  Pallas kernels: 26.3 us -> 25.7 us
    reshape x0 -> x3, local copies, waits for them, and re-layouts: none -> 2.49 us  [the longest x1 1.3 us: fused_local(): sea_mask.reshape(1, cells)]
    unnamed x8, local copies, waits for them, and re-layouts: 3.12 us -> 2.04 us
    convert_element_type x1 -> x0, other arithmetic: 0.71 us -> none  [fused_local(): sea_mask.astype(jnp.float32)]
    pallas_call x1, Pallas kernels: 26.3 us -> 25.7 us  [fused_local(): pl.pallas_call(functools.partial(fused_kernel, count, group), out_shape=(...]
    another operation x1 -> x0, other arithmetic: 0.63 us -> none  [fused_local(): jnp.stack([sea_mask.astype(jnp.float32), wind_speed * jnp.cos(wind_angle)...]
where the time goes in v2:
time: 33 us; the launch traced here: 32.6 us
  Pallas kernels  25.7 us (78%)
  local copies, waits for them, and re-layouts  4.52 us (14%)
  between operations  2.47 us (7%)
    pallas_call x1, Pallas kernels, fused_local(): pl.pallas_call(functools.partial(fused_kernel, count, group), out_shape=(...  25.7 us
    unnamed x8, local copies, waits for them, and re-layouts  2.04 us
    reshape x1, local copies, waits for them, and re-layouts, fused_local(): sea_mask.reshape(1, cells)  1.3 us

profile of v2, /device:TPU:0, one launch (start us, length us, event | category | flops | bytes accessed | tf_op | source)
XLA Modules:
  0.0 32.6 jit_solution(17018657661007886541)
XLA Ops:
  0.6 0.0 copy-start
  0.6 1.3 %reshape.21.sea_in = s32[1,1536]{1,0:T(1,128)} reshape(s32[1536]{0:T(1024)} %param.5) | data formatting | bytes 12288 | tf_op jit(solution)/shard_map/reshape | solution.py:533
  1.9 0.0 copy-done
  1.9 0.0 copy-start.1
  1.9 0.6 %reshape.22.wind_in = f32[1,1536]{1,0:T(1,128)} reshape(f32[1536]{0:T(1024)S(1)} %copy-done) | data formatting | bytes 12288 | tf_op jit(solution)/shard_map/reshape | solution.py:534
  2.5 0.1 copy-done.1
  2.6 0.6 %reshape.23.angle_in = f32[1,1536]{1,0:T(1,128)} reshape(f32[1536]{0:T(1024)S(1)} %copy-done.1) | data formatting | bytes 12288 | tf_op jit(solution)/shard_map/reshape | solution.py:535
  3.2 25.7 %shard_map.67 = (f32[96,1536]{1,0:T(8,128)S(1)}, f32[1,96]{1,0:T(1,128)}, f32[1,1]{1,0:T(1,128)}) custom-call(s32[1,1536]{1,0:T(1,128)} %reshape.21.sea_in, f32[1,1536]{1,0:T(1,128)} %reshape.22.wind_in, f32[1,1536]{1,0:T(1,128)} %reshape.23.angle_in, f32[96,1536]{1,0:T(8,128)} %spec_ref.1), custom_call_target="tpu_custom_call" | custom-call | tf_op jit(solution)/shard_map/pallas_call | solution.py:488
  28.9 0.8 %copy.10 = f32[96,1536]{1,0:T(8,128)} copy(f32[96,1536]{1,0:T(8,128)S(1)} %get-tuple-element.9) | data formatting | bytes 1179648
  29.7 0.0 copy-start.2
  29.7 0.6 %copy-done.2 = f32[1,96]{1,0:T(1,128)S(1)} copy-done((f32[1,96]{1,0:T(1,128)S(1)}, f32[1,96]{1,0:T(1,128)}, u32[]{:S(2)}) %copy-start.2) | copy-done | bytes 408
  30.3 0.5 %copy.11 = f32[96]{0:T(128)} copy(f32[96]{0:T(128)S(1)} %bitcast.2) | data formatting | bytes 768
Async XLA Ops:
  0.6 1.3 %copy-start = (f32[1536]{0:T(1024)S(1)}, f32[1536]{0:T(1024)}, u32[]{:S(2)}) copy-start(f32[1536]{0:T(1024)} %param.6) | copy-start | bytes 18436
  1.9 0.7 %copy-start.1 = (f32[1536]{0:T(1024)S(1)}, f32[1536]{0:T(1024)}, u32[]{:S(2)}) copy-start(f32[1536]{0:T(1024)} %param.7) | copy-start | bytes 18436
  29.7 0.6 %copy-start.2 = (f32[1,96]{1,0:T(1,128)S(1)}, f32[1,96]{1,0:T(1,128)}, u32[]{:S(2)}) copy-start(f32[1,96]{1,0:T(1,128)} %get-tuple-element.7) | copy-start | bytes 1156

commit v3 on v2

--- a/solution.py
+++ b/solution.py
@@ -141,7 +141,7 @@
 
 def fused_kernel(
     count, group, sea_in, wind_in, angle_in, spec_ref, out_ref, wave_ref, mean_ref,
-    sea_raw, wind_raw, aux_ref, aux_sem,
+    sea_raw, wind_raw, angle_raw, aux_ref, aux_sem,
     raw, adv, held, done, mom_out, mom_in, wind, acc, sum_out, sum_in,
     load_sem, held_sem, y_sem, up_sem, down_sem, mom_send, mom_recv,
     ret_send, ret_recv, sum_send, sum_recv,
@@ -178,8 +178,8 @@
     ]
     small = [
         pltpu.make_async_copy(sea_in, sea_raw, aux_sem.at[0]),
-        pltpu.make_async_copy(wind_in, wind_raw.at[0:1], aux_sem.at[1]),
-        pltpu.make_async_copy(angle_in, wind_raw.at[1:2], aux_sem.at[2]),
+        pltpu.make_async_copy(wind_in, wind_raw, aux_sem.at[1]),
+        pltpu.make_async_copy(angle_in, angle_raw, aux_sem.at[2]),
     ]
     for load in small[:1] + loads + small[1:]:
         load.start()
@@ -198,7 +198,7 @@
     log_step = math.log(1.1)
     lats = [math.radians(-75.0 + 150.0 * (r + 0.5) / lat_count) for r in range(lat_count)]
     small[0].wait()
-    aux_ref[0:1] = sea_raw[...].astype(f32)
+    aux_ref[...] = sea_raw[...].astype(f32).reshape(1, cells)
     sea = [aux_ref[0:1, r * NLON : (r + 1) * NLON] for r in range(lat_count)]
     quarter = ND // 4
     tiles = NLON // LANES
@@ -280,7 +280,8 @@
 
     small[1].wait()
     small[2].wait()
-    speed_own, angle_own = wind_raw[0:1, cells_of(rank)], wind_raw[1:2, cells_of(rank)]
+    speed_own = wind_raw[cells_of(rank)].reshape(1, width)
+    angle_own = angle_raw[cells_of(rank)].reshape(1, width)
     wind[...] = jnp.concatenate([cos_h] * (width // LANES), axis=1) * (
         speed_own * jnp.cos(angle_own)
     ) + jnp.concatenate([sin_h] * (width // LANES), axis=1) * (speed_own * jnp.sin(angle_own))
@@ -444,7 +445,7 @@
     points = cells // count
     shift = (me % per_row) * points
     turned = pltpu.roll(jnp.broadcast_to(mine, (8, width)), (width - shift) % width, 1)
-    wave_ref[...] = turned[0:1, :points]
+    wave_ref[...] = turned[0, :points]
     mean_ref[...] = jnp.sum(height_sum, axis=1, keepdims=True) * (1.0 / (SEA_DEV * count))
 
     for f in range(freq_dev):
@@ -489,7 +490,7 @@
         functools.partial(fused_kernel, count, group),
         out_shape=(
             pltpu.VMEM((bins_dev, cells), f32),
-            jax.ShapeDtypeStruct((1, points), f32),
+            pltpu.VMEM((points,), f32),
             jax.ShapeDtypeStruct((1, 1), f32),
         ),
         in_specs=[
@@ -502,8 +503,9 @@
             pl.BlockSpec(memory_space=pltpu.VMEM),
         ),
         scratch_shapes=[
-            pltpu.VMEM((1, cells), jnp.int32),
-            pltpu.VMEM((2, cells), f32),
+            pltpu.VMEM((cells,), jnp.int32),
+            pltpu.VMEM((cells,), f32),
+            pltpu.VMEM((cells,), f32),
             pltpu.VMEM((1, cells), f32),
             dma((3,)),
             pltpu.VMEM((bins_dev, cells), f32),
@@ -529,13 +531,8 @@
             dma((count,)),
         ],
         compiler_params=pltpu.CompilerParams(collective_id=0, has_side_effects=True),
-    )(
-        sea_mask.reshape(1, cells),
-        wind_speed.reshape(1, cells),
-        wind_angle.reshape(1, cells),
-        spectrum,
-    )
-    return (out, wave.reshape(points), mean.reshape(1))
+    )(sea_mask, wind_speed, wind_angle, spectrum)
+    return (out, wave, mean.reshape(1))
 
 
 def solution(mesh):

time: 33 us -> 29.5 us (0.89)
  local copies, waits for them, and re-layouts: 4.52 us -> 1.33 us
    reshape x3 -> x0, local copies, waits for them, and re-layouts: 2.49 us -> none  [the longest x1 1.3 us: fused_local(): sea_mask.reshape(1, cells)]
    unnamed x8 -> x2, local copies, waits for them, and re-layouts: 2.04 us -> 1.33 us
where the time goes in v3:
time: 29.5 us; the launch traced here: 29.3 us
  Pallas kernels  25.6 us (87%)
  between operations  2.33 us (8%)
  local copies, waits for them, and re-layouts  1.33 us (5%)
    pallas_call x1, Pallas kernels, fused_local(): pl.pallas_call(functools.partial(fused_kernel, count, group), out_shape=(...  25.6 us
    unnamed x2, local copies, waits for them, and re-layouts  1.33 us

profile of v3, /device:TPU:0, one launch (start us, length us, event | category | flops | bytes accessed | tf_op | source)
XLA Modules:
  0.0 29.3 jit_solution(14951112003680783689)
XLA Ops:
  0.6 25.6 %shard_map.67 = (f32[96,1536]{1,0:T(8,128)S(1)}, f32[96]{0:T(128)S(1)}, f32[1,1]{1,0:T(1,128)}) custom-call(s32[1536]{0:T(1024)} %sea_in.1, f32[1536]{0:T(1024)} %wind_in.1, f32[1536]{0:T(1024)} %angle_in.1, f32[96,1536]{1,0:T(8,128)} %spec_ref.1), custom_call_target="tpu_custom_call" | custom-call | tf_op jit(solution)/shard_map/pallas_call | solution.py:489
  26.3 0.8 %copy.10 = f32[96,1536]{1,0:T(8,128)} copy(f32[96,1536]{1,0:T(8,128)S(1)} %get-tuple-element.9) | data formatting | bytes 1179648
  27.1 0.5 %copy.11 = f32[96]{0:T(128)} copy(f32[96]{0:T(128)S(1)} %get-tuple-element.10) | data formatting | bytes 768

commit v4 on v3

--- a/solution.py
+++ b/solution.py
@@ -147,8 +147,7 @@
     ret_send, ret_recv, sum_send, sum_recv,
 ):
     f32 = jnp.float32
-    bins_dev, cells = adv.shape
-    freq_dev = bins_dev // ND
+    freq_dev, _, cells = adv.shape
     freq_group = freq_dev * group
     width = cells // group
     zones = count // group
@@ -191,6 +190,39 @@
     @pl.when(zone == zones - 1)
     def _():
         held[HALO + freq_group :] = jnp.zeros((HALO, ND, width), f32)
+
+    def cells_of(index):
+        return pl.ds(pl.multiple_of(index * width, LANES), width)
+
+    def tile_of(index, t):
+        return pl.ds(pl.multiple_of(index * width + t * LANES, LANES), LANES)
+
+    def lanes_of(t):
+        return pl.ds(t * LANES, LANES)
+
+    offsets = [(dy, dc) for dy in range(sides) for dc in range(2)]
+
+    def rank_of(offset):
+        return (side + offset[0]) % sides * 2 + (core + offset[1]) % 2
+
+    def y_copy(f, i, t):
+        peer = rank_of(offsets[i])
+        slot = HALO + rank * freq_dev + f
+        return remote(
+            adv.at[f, :, tile_of(peer, t)], held.at[slot, :, lanes_of(t)],
+            y_sem.at[i - 1, f, t], held_sem.at[slot, t], zone * group + peer,
+        )
+
+    def own_copy(f, t):
+        slot = HALO + rank * freq_dev + f
+        return pltpu.make_async_copy(
+            adv.at[f, :, tile_of(rank, t)], held.at[slot, :, lanes_of(t)], held_sem.at[slot, t]
+        )
+
+    def y_start(f, t):
+        for i in list(range(2, group)) + [1]:
+            y_copy(f, i, t).start()
+        own_copy(f, t).start()
 
     dirs = lax.broadcasted_iota(jnp.int32, (ND, LANES), 0).astype(f32)
     heading = 2.0 * math.pi * (dirs + 0.5) / ND
@@ -202,6 +234,7 @@
     sea = [aux_ref[0:1, r * NLON : (r + 1) * NLON] for r in range(lat_count)]
     quarter = ND // 4
     tiles = NLON // LANES
+    parts = width // LANES
     moments = [[jnp.zeros((quarter, NLON), f32) for _ in range(lat_count)] for _ in range(2)]
     for f in range(freq_dev):
         loads[f].wait()
@@ -228,21 +261,20 @@
                     fresh.append((e - cx[r] * (e - side_x) - cy * (e - side_y)) * sea[r])
                 energy = fresh
             for r in range(lat_count):
-                adv[rows, r * NLON : (r + 1) * NLON] = energy[r]
+                adv[f, part, r * NLON : (r + 1) * NLON] = energy[r]
                 sums[r] = energy[r] if q == 0 else sums[r] + energy[r]
         for r in range(lat_count):
             moments[0][r] = moments[0][r] + sums[r]
             moments[1][r] = moments[1][r] + omega * sums[r]
+        if f == 0:
+            pl.semaphore_wait(barrier, count - 1)
+        if f < freq_dev - 1:
+            y_start(f, 0)
     for i in range(2):
         for r in range(lat_count):
             mom_out[i : i + 1, r * NLON : (r + 1) * NLON] = jnp.sum(
                 moments[i][r], axis=0, keepdims=True
             )
-
-    pl.semaphore_wait(barrier, count - 1)
-
-    def cells_of(index):
-        return pl.ds(pl.multiple_of(index * width, LANES), width)
 
     for step in range(1, count):
         target = (me + step) % count
@@ -250,33 +282,14 @@
             mom_out.at[:, cells_of(target % group)], mom_in.at[me],
             mom_send.at[step - 1], mom_recv.at[me], target,
         ).start()
-
-    offsets = [(dy, dc) for dy in range(sides) for dc in range(2)]
-
-    def rank_of(offset):
-        return (side + offset[0]) % sides * 2 + (core + offset[1]) % 2
-
-    def y_copy(f, i):
-        peer = rank_of(offsets[i])
-        return remote(
-            adv.at[pl.ds(f * ND, ND), cells_of(peer)], held.at[HALO + rank * freq_dev + f],
-            y_sem.at[i - 1, f], held_sem.at[HALO + rank * freq_dev + f], zone * group + peer,
-        )
-
-    def own_copy(f):
-        slot = HALO + rank * freq_dev + f
-        return pltpu.make_async_copy(
-            adv.at[pl.ds(f * ND, ND), cells_of(rank)], held.at[slot], held_sem.at[slot]
-        )
-
-    for f in range(freq_dev):
-        for i in list(range(2, group)) + [1]:
-            y_copy(f, i).start()
-        own_copy(f).start()
     local_mom = pltpu.make_async_copy(
         mom_out.at[:, cells_of(rank)], mom_in.at[me], mom_recv.at[me]
     )
     local_mom.start()
+    y_start(freq_dev - 1, 0)
+    for t in range(1, parts):
+        for f in range(freq_dev):
+            y_start(f, t)
 
     small[1].wait()
     small[2].wait()
@@ -286,42 +299,51 @@
         speed_own * jnp.cos(angle_own)
     ) + jnp.concatenate([sin_h] * (width // LANES), axis=1) * (speed_own * jnp.sin(angle_own))
 
-    def up_copy(slot):
+    def up_copy(slot, t):
         return remote(
-            held.at[HALO + slot], held.at[HALO + slot - freq_group],
-            up_sem.at[slot - (freq_group - HALO)], held_sem.at[HALO + slot - freq_group],
+            held.at[HALO + slot, :, lanes_of(t)],
+            held.at[HALO + slot - freq_group, :, lanes_of(t)],
+            up_sem.at[slot - (freq_group - HALO), t],
+            held_sem.at[HALO + slot - freq_group, t],
             (zone + 1) % zones * group + rank,
         )
 
-    def down_copy(slot):
+    def down_copy(slot, t):
         return remote(
-            held.at[HALO + slot], held.at[HALO + slot + freq_group],
-            down_sem.at[slot], held_sem.at[HALO + slot + freq_group],
+            held.at[HALO + slot, :, lanes_of(t)],
+            held.at[HALO + slot + freq_group, :, lanes_of(t)],
+            down_sem.at[slot, t],
+            held_sem.at[HALO + slot + freq_group, t],
             (zone + zones - 1) % zones * group + rank,
         )
 
-    def arrive(index):
+    def arrive(index, t):
+        block = held.at[index, :, lanes_of(t)]
         remote(
-            held.at[index], held.at[index], up_sem.at[0], held_sem.at[index],
-            (me + 1) % count,
+            block, block, up_sem.at[0, t], held_sem.at[index, t], (me + 1) % count
         ).wait_recv()
 
-    for dy in range(sides):
+    def arrive_group(dy, t):
         for f in range(freq_dev):
             for dc in range(2):
                 slot = rank_of((dy, dc)) * freq_dev + f
                 if (dy, dc) == (0, 0):
-                    own_copy(f).wait()
+                    own_copy(f, t).wait()
                 else:
-                    arrive(HALO + slot)
+                    arrive(HALO + slot, t)
 
                 @pl.when((slot >= freq_group - HALO) & (zone < zones - 1))
                 def _():
-                    up_copy(slot).start()
+                    up_copy(slot, t).start()
 
                 @pl.when((slot < HALO) & (zone > 0))
                 def _():
-                    down_copy(slot).start()
+                    down_copy(slot, t).start()
+
+    for t in range(parts):
+        arrive_group(0, t)
+    for dy in range(1, sides):
+        arrive_group(dy, 0)
 
     local_mom.wait()
     for step in range(1, count):
@@ -338,48 +360,41 @@
     acc[...] = jnp.zeros_like(acc)
     ascending = side > 0
 
-    for i in range(HALO):
-        early = jnp.where(ascending, i, HALO + freq_group + i)
-
-        @pl.when(jnp.where(ascending, zone > 0, zone < zones - 1))
+    def arrive_halo(at_top, t):
+        @pl.when(jnp.where(at_top, zone < zones - 1, zone > 0))
         def _():
-            arrive(early)
-
-    def ret_copy(k):
-        owner, f = k // freq_dev, k % freq_dev
+            for i in range(HALO):
+                arrive(jnp.where(at_top, HALO + freq_group + i, i), t)
+
+    def ret_copy(owner, t):
         return remote(
-            done.at[k],
-            out_ref.at[pl.ds(pl.multiple_of(f * ND, ND), ND), cells_of(rank)],
-            ret_send.at[k], ret_recv.at[rank, f], zone * group + owner,
-        )
-
-    def ret_local(k):
-        f = k % freq_dev
+            done.at[pl.ds(owner * freq_dev, freq_dev), :, lanes_of(t)],
+            out_ref.at[:, :, tile_of(rank, t)],
+            ret_send.at[owner, t], ret_recv.at[rank, t], zone * group + owner,
+        )
+
+    def ret_local(t):
         return pltpu.make_async_copy(
-            done.at[k],
-            out_ref.at[pl.ds(pl.multiple_of(f * ND, ND), ND), cells_of(rank)],
-            ret_recv.at[rank, f],
-        )
-
-    def source_step(i, carry):
-        k = jnp.where(ascending, i, freq_group - 1 - i)
-        late = i - (freq_group - HALO)
-
-        @pl.when((late >= 0) & jnp.where(ascending, zone < zones - 1, zone > 0))
-        def _():
-            arrive(jnp.where(ascending, HALO + freq_group + late, HALO - 1 - late))
-
-        freq = zone * freq_group + k
-
-        def scale(index, factor):
-            return jnp.where((index >= 3) & (index <= NF - 3), factor, 0.0).astype(f32)
-
-        w_own, w_low, w_high = scale(freq, -0.002), scale(freq - 2, 0.001), scale(freq + 3, 0.001)
-        omega = jnp.exp(
-            jnp.full((1, LANES), log_step, f32) * (freq.astype(f32) - NF // 2)
-        )
-        for t in range(width // LANES):
-            lanes = slice(t * LANES, (t + 1) * LANES)
+            done.at[pl.ds(rank * freq_dev, freq_dev), :, lanes_of(t)],
+            out_ref.at[:, :, tile_of(rank, t)],
+            ret_recv.at[rank, t],
+        )
+
+    def sources(t, begin, end):
+        lanes = slice(t * LANES, (t + 1) * LANES)
+
+        def source_step(i, carry):
+            k = jnp.where(ascending, i, freq_group - 1 - i)
+            freq = zone * freq_group + k
+
+            def scale(index, factor):
+                return jnp.where((index >= 3) & (index <= NF - 3), factor, 0.0).astype(f32)
+
+            w_own = scale(freq, -0.002)
+            w_low, w_high = scale(freq - 2, 0.001), scale(freq + 3, 0.001)
+            omega = jnp.exp(
+                jnp.full((1, LANES), log_step, f32) * (freq.astype(f32) - NF // 2)
+            )
 
             def slab(shift):
                 return held[HALO + k + shift, :, lanes]
@@ -391,7 +406,7 @@
                 return a * (a * (p + m) - 2.0 * (p * m))
 
             own = slab(0)
-            p2, m3, m2, m5, p3, p5 = (slab(s) for s in (2, -3, -2, -5, 3, 5))
+            p2, m3, m2, m5, p3, p5 = (slab(shift) for shift in (2, -3, -2, -5, 3, 5))
             near = rate(own, turn(p2, -1), turn(m3, 3)) + rate(own, turn(p2, 1), turn(m3, -3))
             low = rate(turn(m2, 1), own, turn(m5, 4)) + rate(turn(m2, -1), own, turn(m5, -4))
             high = rate(turn(p3, -3), turn(p5, -4), own) + rate(turn(p3, 3), turn(p5, 4), own)
@@ -401,18 +416,33 @@
             fresh = own + (gain - damping) * own + interaction
             done[k, :, lanes] = fresh
             acc[:, lanes] += fresh
-
-        @pl.when(k // freq_dev == rank)
-        def _():
-            ret_local(k).start()
-
-        @pl.when(k // freq_dev != rank)
-        def _():
-            ret_copy(k).start()
-
-        return carry
-
-    lax.fori_loop(0, freq_group, source_step, 0)
+            return carry
+
+        lax.fori_loop(begin, end, source_step, 0)
+
+    half = freq_group // 2
+    near_side = rank_of((0, 1))
+
+    def first_half(t):
+        arrive_halo(jnp.logical_not(ascending), t)
+        sources(t, 0, half)
+        for dy in range(1, sides):
+            for dc in range(2):
+                ret_copy(rank_of((dy, dc)), t).start()
+
+    def second_half(t):
+        arrive_halo(ascending, t)
+        sources(t, half, freq_group)
+        ret_copy(near_side, t).start()
+        ret_local(t).start()
+
+    first_half(0)
+    for t in range(1, parts):
+        for dy in range(1, sides):
+            arrive_group(dy, t)
+        first_half(t)
+        second_half(t - 1)
+    second_half(parts - 1)
 
     sum_out[...] = jnp.sum(acc[...], axis=0, keepdims=True)
 
@@ -448,16 +478,17 @@
     wave_ref[...] = turned[0, :points]
     mean_ref[...] = jnp.sum(height_sum, axis=1, keepdims=True) * (1.0 / (SEA_DEV * count))
 
-    for f in range(freq_dev):
+    for t in range(parts):
         for i in range(1, group):
             peer = rank_of(offsets[i])
             remote(
-                done.at[0], out_ref.at[pl.ds(f * ND, ND), cells_of(peer)],
-                ret_send.at[0], ret_recv.at[peer, f], zone * group + peer,
+                done.at[pl.ds(0, freq_dev), :, lanes_of(t)], out_ref.at[:, :, tile_of(peer, t)],
+                ret_send.at[peer, t], ret_recv.at[peer, t], zone * group + peer,
             ).wait_recv()
-            y_copy(f, i).wait_send()
-            ret_copy(peer * freq_dev + f).wait_send()
-        ret_local(rank * freq_dev + f).wait()
+            for f in range(freq_dev):
+                y_copy(f, i, t).wait_send()
+            ret_copy(peer, t).wait_send()
+        ret_local(t).wait()
     for step in range(1, count):
         remote(
             mom_out.at[:, cells_of(0)], mom_in.at[me], mom_send.at[step - 1],
@@ -467,13 +498,15 @@
 
     @pl.when(zone < zones - 1)
     def _():
-        for slot in range(freq_group - HALO, freq_group):
-            up_copy(slot).wait_send()
+        for t in range(parts):
+            for slot in range(freq_group - HALO, freq_group):
+                up_copy(slot, t).wait_send()
 
     @pl.when(zone > 0)
     def _():
-        for slot in range(HALO):
-            down_copy(slot).wait_send()
+        for t in range(parts):
+            for slot in range(HALO):
+                down_copy(slot, t).wait_send()
 
 
 def fused_local(spectrum, sea_mask, wind_speed, wind_angle):
@@ -484,12 +517,13 @@
     freq_group = freq_dev * group
     width = cells // group
     points = cells // count
+    parts = width // LANES
     f32 = jnp.float32
     dma = pltpu.SemaphoreType.DMA
     out, wave, mean = pl.pallas_call(
         functools.partial(fused_kernel, count, group),
         out_shape=(
-            pltpu.VMEM((bins_dev, cells), f32),
+            pltpu.VMEM((freq_dev, ND, cells), f32),
             pltpu.VMEM((points,), f32),
             jax.ShapeDtypeStruct((1, 1), f32),
         ),
@@ -509,7 +543,7 @@
             pltpu.VMEM((1, cells), f32),
             dma((3,)),
             pltpu.VMEM((bins_dev, cells), f32),
-            pltpu.VMEM((bins_dev, cells), f32),
+            pltpu.VMEM((freq_dev, ND, cells), f32),
             pltpu.VMEM((freq_group + 2 * HALO, ND, width), f32),
             pltpu.VMEM((freq_group, ND, width), f32),
             pltpu.VMEM((2, cells), f32),
@@ -519,20 +553,20 @@
             pltpu.VMEM((1, width), f32),
             pltpu.VMEM((count, 1, width), f32),
             dma((freq_dev,)),
-            dma((freq_group + 2 * HALO,)),
-            dma((group - 1, freq_dev)),
-            dma((HALO,)),
-            dma((HALO,)),
+            dma((freq_group + 2 * HALO, parts)),
+            dma((group - 1, freq_dev, parts)),
+            dma((HALO, parts)),
+            dma((HALO, parts)),
             dma((count - 1,)),
             dma((count,)),
-            dma((freq_group,)),
-            dma((group, freq_dev)),
+            dma((group, parts)),
+            dma((group, parts)),
             dma((count - 1,)),
             dma((count,)),
         ],
         compiler_params=pltpu.CompilerParams(collective_id=0, has_side_effects=True),
     )(sea_mask, wind_speed, wind_angle, spectrum)
-    return (out, wave, mean.reshape(1))
+    return (out.reshape(bins_dev, cells), wave, mean.reshape(1))
 
 
 def solution(mesh):

time: 29.5 us -> 27.6 us (0.936)
  Pallas kernels: 25.6 us -> 23.8 us
    pallas_call x1, Pallas kernels: 25.6 us -> 23.8 us  [fused_local(): pl.pallas_call(functools.partial(fused_kernel, count, group), out_shape=(...]
where the time goes in v4:
time: 27.6 us; the launch traced here: 27.4 us
  Pallas kernels  23.8 us (86%)
  between operations  2.33 us (8%)
  local copies, waits for them, and re-layouts  1.33 us (5%)
    pallas_call x1, Pallas kernels, fused_local(): pl.pallas_call(functools.partial(fused_kernel, count, group), out_shape=(...  23.8 us
    unnamed x2, local copies, waits for them, and re-layouts  1.33 us

profile of v4, /device:TPU:0, one launch (start us, length us, event | category | flops | bytes accessed | tf_op | source)
XLA Modules:
  0.0 27.4 jit_solution(12750963219816293330)
XLA Ops:
  0.6 23.8 %shard_map.67 = (f32[3,32,1536]{2,1,0:T(8,128)S(1)}, f32[96]{0:T(128)S(1)}, f32[1,1]{1,0:T(1,128)}) custom-call(s32[1536]{0:T(1024)} %sea_in.1, f32[1536]{0:T(1024)} %wind_in.1, f32[1536]{0:T(1024)} %angle_in.1, f32[96,1536]{1,0:T(8,128)} %spec_ref.1), custom_call_target="tpu_custom_call" | custom-call | tf_op jit(solution)/shard_map/pallas_call | solution.py:523
  24.4 0.8 %copy.10 = f32[96,1536]{1,0:T(8,128)} copy(f32[96,1536]{1,0:T(8,128)S(1)} %bitcast.2) | data formatting | bytes 1179648
  25.2 0.5 %copy.11 = f32[96]{0:T(128)} copy(f32[96]{0:T(128)S(1)} %get-tuple-element.10) | data formatting | bytes 768

commit v5 on v4

--- a/solution.py
+++ b/solution.py
@@ -507,6 +507,17 @@
         for t in range(parts):
             for slot in range(HALO):
                 down_copy(slot, t).wait_send()
+
+
+def store_kernel(new_in, wave_in, new_out, wave_out, sem):
+    copies = [
+        pltpu.make_async_copy(new_in, new_out, sem.at[0]),
+        pltpu.make_async_copy(wave_in, wave_out, sem.at[1]),
+    ]
+    for copy in copies:
+        copy.start()
+    for copy in copies:
+        copy.wait()
 
 
 def fused_local(spectrum, sea_mask, wind_speed, wind_angle):
@@ -566,6 +577,19 @@
         ],
         compiler_params=pltpu.CompilerParams(collective_id=0, has_side_effects=True),
     )(sea_mask, wind_speed, wind_angle, spectrum)
+    out, wave = pl.pallas_call(
+        store_kernel,
+        out_shape=(
+            pltpu.HBM(out.shape, f32),
+            pltpu.HBM(wave.shape, f32),
+        ),
+        in_specs=[pl.BlockSpec(memory_space=pltpu.VMEM)] * 2,
+        out_specs=(pl.BlockSpec(memory_space=pltpu.HBM),) * 2,
+        scratch_shapes=[dma((2,))],
+    )(
+        pltpu.with_memory_space_constraint(out, pltpu.VMEM),
+        pltpu.with_memory_space_constraint(wave, pltpu.VMEM),
+    )
     return (out.reshape(bins_dev, cells), wave, mean.reshape(1))
 
 

time: 27.6 us -> 27.3 us (0.989)
  local copies, waits for them, and re-layouts: 1.33 us -> 0 us
  Pallas kernels: 23.8 us -> 24.7 us
    unnamed x2 -> x0, local copies, waits for them, and re-layouts: 1.33 us -> none
    pallas_call x0 -> x1, Pallas kernels: none -> 0.84 us  [fused_local(): pl.pallas_call(store_kernel, out_shape=(pltpu.HBM(out.shape, f32), pltpu....]
where the time goes in v5:
time: 27.3 us; the launch traced here: 27.1 us
  Pallas kernels  24.7 us (90%)
  between operations  2.4 us (9%)
    pallas_call x1, Pallas kernels, fused_local(): pl.pallas_call(functools.partial(fused_kernel, count, group), out_shape=(...  23.8 us
    pallas_call x1, Pallas kernels, fused_local(): pl.pallas_call(store_kernel, out_shape=(pltpu.HBM(out.shape, f32), pltpu....  0.84 us

profile of v5, /device:TPU:0, one launch (start us, length us, event | category | flops | bytes accessed | tf_op | source)
XLA Modules:
  0.0 27.1 jit_solution(12575389638370426129)
XLA Ops:
  0.6 23.8 %shard_map.67 = (f32[3,32,1536]{2,1,0:T(8,128)S(1)}, f32[96]{0:T(128)S(1)}, f32[1,1]{1,0:T(1,128)}) custom-call(s32[1536]{0:T(1024)} %sea_in.1, f32[1536]{0:T(1024)} %wind_in.1, f32[1536]{0:T(1024)} %angle_in.1, f32[96,1536]{1,0:T(8,128)} %spec_ref.1), custom_call_target="tpu_custom_call" | custom-call | tf_op jit(solution)/shard_map/pallas_call | solution.py:534
  24.5 0.8 %shard_map.68 = (f32[3,32,1536]{2,1,0:T(8,128)}, f32[96]{0:T(128)}) custom-call(f32[3,32,1536]{2,1,0:T(8,128)S(1)} %get-tuple-element.8.new_in, f32[96]{0:T(128)S(1)} %get-tuple-element.9.wave_in), custom_call_target="tpu_custom_call" | custom-call | tf_op jit(solution)/shard_map/pallas_call | solution.py:580
